TPU v7x, 32 devices: a whole 2x2x4 slice. The times are simulated.
32 devices in a mesh: ia: 4 (over y, x), ja: 4 (over z), col: 2 (over core).
Axes of the slice: x: 2, y: 2, z: 4, core: 2. Of those that a mesh axis runs over, the one named last changes fastest.
Arguments:
- pair_rep: bfloat16 [512, 512, 128], P('ia', 'ja'), may hold values from -6 to 6
- norm_gain: float32 [128], replicated, may hold values from 0.1 to 1.9
- weights: bfloat16 [4, 128, 128], P(None, None, 'col'), may hold values from -0.5 to 0.5
- residue_mask: int32 [512], replicated, may hold values 0 or 1
- product_grad: bfloat16 [512, 128, 512], P('ia', 'col', 'ja'), may hold values from -1 to 1
Outputs:
- pair_grad: bfloat16 [512, 512, 128], P('ia', 'ja')
- weight_grads: float32 [4, 128, 128], P(None, None, 'col')
All inputs are finite; a program needn't handle non-finite values.
Results may differ from a plain program's by a relative error of at most 0.0067.
Values may be sent and summed in bfloat16 or wider, within the bound.
A program may use at most 128 MiB of HBM per device.

v0:
```python
import jax
import jax.numpy as jnp
from jax import lax
from jax.sharding import PartitionSpec as P

CLIP_LIMIT = 64.0


def gate_terms(incoming, linear, gate_pre, pair_valid):
    sigmoid_gate = jax.nn.sigmoid(gate_pre)
    through = incoming * pair_valid
    return (through * sigmoid_gate, through * linear * sigmoid_gate * (1.0 - sigmoid_gate))


def on_device(pair_rep, norm_gain, weights, residue_mask, product_grad):
    row_count = pair_rep.shape[0]
    col_count = pair_rep.shape[1]
    row_first = lax.axis_index("ia") * row_count
    col_first = lax.axis_index("ja") * col_count
    validity = residue_mask.astype(jnp.float32)
    row_valid = lax.dynamic_slice_in_dim(validity, row_first, row_count)
    col_valid = lax.dynamic_slice_in_dim(validity, col_first, col_count)
    pair_valid = row_valid[:, None, None] * col_valid[None, None, :]
    floats = pair_rep.astype(jnp.float32)
    centred = floats - jnp.mean(floats, axis=-1, keepdims=True)
    inv_std = lax.rsqrt(jnp.mean(centred * centred, axis=-1, keepdims=True) + 1e-05)
    unit_rows = centred * inv_std
    normed = (unit_rows * norm_gain).astype(jnp.bfloat16)
    projected = jnp.einsum("ikd,wdc->wick", normed, weights, preferred_element_type=jnp.float32)
    left_side = (pair_valid * jax.nn.sigmoid(projected[1]) * projected[0]).astype(jnp.bfloat16)
    right_side = (pair_valid * jax.nn.sigmoid(projected[3]) * projected[2]).astype(jnp.bfloat16)
    row_panel = lax.all_gather(product_grad, "ja", axis=2, tiled=True)
    panel_part = row_panel
    grad_left = jnp.einsum(
        "icj,jck->ick",
        panel_part,
        lax.all_gather(right_side, "ia", axis=0, tiled=True),
        preferred_element_type=jnp.float32,
    )
    panel_part = row_panel
    grad_right = lax.psum_scatter(
        jnp.einsum("icj,ick->jck", panel_part, left_side, preferred_element_type=jnp.float32),
        "ia",
        scatter_dimension=0,
        tiled=True,
    )
    lin_a, gate_a = gate_terms(grad_left, projected[0], projected[1], pair_valid)
    lin_b, gate_b = gate_terms(grad_right, projected[2], projected[3], pair_valid)
    proj_grads = jnp.stack([lin_a, gate_a, lin_b, gate_b]).astype(jnp.bfloat16)
    grad_part = jnp.einsum("ikd,wick->wdc", normed, proj_grads, preferred_element_type=jnp.float32)
    input_part = jnp.einsum(
        "wick,wdc->ikd", proj_grads, weights, preferred_element_type=jnp.float32
    )
    normed_grad = lax.psum(input_part, "col")
    scaled = normed_grad * norm_gain
    pair_grad = inv_std * (
        scaled
        - jnp.mean(scaled, axis=-1, keepdims=True)
        - unit_rows * jnp.mean(scaled * unit_rows, axis=-1, keepdims=True)
    )
    summed = lax.psum(grad_part, ("ia", "ja"))
    squares = lax.psum(jnp.sum(summed * summed), "col")
    factor = jnp.minimum(1.0, CLIP_LIMIT * lax.rsqrt(squares + 1e-06))
    weight_grads = summed * factor
    return (pair_grad.astype(jnp.bfloat16), weight_grads)


def solution(mesh):
    placed = (P("ia", "ja", None), P(), P(None, None, "col"), P(), P("ia", "col", "ja"))
    return jax.shard_map(
        on_device,
        mesh=mesh,
        in_specs=placed,
        out_specs=(P("ia", "ja", None), P(None, None, "col")),
        check_vma=False,
    )
```

profile of v0, /device:TPU:0, one launch (start us, length us, event | category | flops | bytes accessed | tf_op | source)
XLA Modules:
  0.0 660.3 jit_solution(14896707460684824877)
XLA Ops:
  7.2 4.3 copy.18
  11.5 0.0 all-gather.3.cloned.1.call-start
  11.6 0.1 fusion.41
  11.7 0.1 broadcast_multiply_fusion.1
  11.8 3.5 convert_reduce_fusion
  15.3 4.8 fusion.10
  20.2 4.7 convolution_bitcast_fusion
  24.9 5.9 copy-done.1
  30.8 2.6 multiply_convert_fusion.5
  33.4 0.5 reduce-scatter.2.cloned.1.call-start
  33.9 129.6 %all-gather.5.cloned.1.call-done = bf16[128,64,512]{2,0,1:T(8,128)(2,1)} async-done(((bf16[128,64,128]{2,0,1:T(8,128)(2,1)}), bf16[128,64,512]{2,0,1:T(8,128)(2,1)}) %all-gather.5.cloned.1.call-update) | async-done | bytes 8388624 | tf_op jit(solution)/shard_map/all_gather | solution.py:32
  163.5 87.5 %all-gather.3.cloned.1.call-done = bf16[512,64,128]{2,1,0:T(8,128)(2,1)} async-done(((bf16[128,64,128]{2,1,0:T(8,128)(2,1)}), bf16[512,64,128]{2,1,0:T(8,128)(2,1)}) %all-gather.3.cloned.1.call-update) | async-done | bytes 8388624 | tf_op jit(solution)/shard_map/all_gather | solution.py:37
  251.0 25.2 %fusion.11 = f32[64,128,128]{2,1,0:T(8,128)} fusion(bf16[128,64,512]{2,0,1:T(8,128)(2,1)} %all-gather.5.cloned.1.call-done, bf16[512,64,128]{2,1,0:T(8,128)(2,1)} %all-gather.3.cloned.1.call-done), kind=kOutput, calls=%fused_computation.15 | convolution fusion | flops 1073741824 | bytes 20971520 | tf_op jit(solution)/shard_map/icj,jck->ick/dot_general | solution.py:34
  276.2 5.4 copy.20
  281.6 6.8 %fusion.28 = (bf16[1,128,64,128]{3,2,1,0:T(8,128)(2,1)S(1)}, bf16[1,128,64,128]{3,2,1,0:T(8,128)(2,1)}, bf16[128,64,128]{2,1,0:T(8,128)(2,1)S(1)}) fusion(f32[64,128,128]{1,0,2:T(8,128)} %copy.20, f32[128,128]{1,0:T(8,128)S(1)} %broadcast_multiply_fusion.1, f32[4,128,64,128]{3,2,0,1:T(8,128)} %copy-done.1), kind=kLoop, calls=%fused_computation.43 | loop fusion | flops 14680064 | bytes 18939904 | tf_op jit(solution)/shard_map/stack | solution.py:49
  288.5 14.1 %fusion.32 = f32[64,128,512]{2,1,0:T(8,128)} fusion(bf16[128,64,512]{2,0,1:T(8,128)(2,1)} %all-gather.5.cloned.1.call-done, bf16[128,64,128]{2,1,0:T(8,128)(2,1)S(1)} %get-tuple-element.8), kind=kOutput, calls=%fused_computation.47 | convolution fusion | flops 1073741824 | bytes 27262976 | tf_op jit(solution)/shard_map/icj,ick->jck/dot_general | solution.py:42
  302.6 16.6 %copy.23 = f32[64,128,512]{1,0,2:T(8,128)} copy(f32[64,128,512]{2,1,0:T(8,128)} %fusion.32) | data formatting | bytes 33554432 | tf_op jit(solution)/shard_map/icj,ick->jck/dot_general | solution.py:42
  319.2 0.0 all-reduce.5.cloned.1.call-start
  319.2 153.8 %reduce-scatter.2.cloned.1.call-done = f32[128,64,128]{2,1,0:T(8,128)} async-done(((f32[512,64,128]{2,1,0:T(8,128)}), f32[128,64,128]{2,1,0:T(8,128)}) %reduce-scatter.2.cloned.1.call-update) | async-done | bytes 4194320 | tf_op jit(solution)/shard_map/reduce_scatter | solution.py:41
  473.1 6.0 fusion.30
  479.2 1.3 copy-done.7
  480.4 0.7 copy-done.8
  481.1 5.4 fusion.34
  486.6 0.0 all-reduce.3.cloned.1.call-start
  486.6 6.5 convolution_bitcast_fusion.1
  493.1 99.0 %all-reduce.5.cloned.1.call-done = f32[4,128,64]{1,2,0:T(8,128)} async-done(((f32[4,128,64]{1,2,0:T(8,128)}), f32[4,128,64]{1,2,0:T(8,128)}) %all-reduce.5.cloned.1.call-update) | async-done | bytes 131088 | tf_op jit(solution)/shard_map/psum | solution.py:61
  592.1 1.5 multiply_reduce_fusion.1
  593.7 3.1 psum.23
  597.4 1.6 broadcast_multiply_fusion
  599.0 32.2 %all-reduce.3.cloned.1.call-done = f32[128,128,128]{2,1,0:T(8,128)} async-done(((f32[128,128,128]{2,1,0:T(8,128)}), f32[128,128,128]{2,1,0:T(8,128)}) %all-reduce.3.cloned.1.call-update) | async-done | bytes 8388624 | tf_op jit(solution)/shard_map/psum | solution.py:54
  631.2 11.6 %multiply_reduce_fusion = (f32[128,128]{1,0:T(8,128)S(1)}, f32[128,128]{1,0:T(8,128)S(1)}) fusion(f32[128,128,128]{2,1,0:T(8,128)} %all-reduce.3.cloned.1.call-done, f32[128]{0:T(128)S(1)} %copy-done.9, f32[128,128]{1,0:T(8,128)S(1)} %add_rsqrt_fusion, f32[128,128]{1,0:T(8,128)S(1)} %broadcast_multiply_fusion.4, bf16[128,128,128]{2,1,0:T(8,128)(2,1)} %param.5), kind=kLoop, calls=%fused_computation.17 | loop fusion | flops 14647296 | bytes 12845568 | tf_op jit(solution)/shard_map/reduce_sum | solution.py:58
  642.8 10.7 %fusion.9 = bf16[128,128,128]{2,1,0:T(8,128)(2,1)} fusion(bf16[128,128,128]{2,1,0:T(8,128)(2,1)S(1)} %copy-done.4, f32[128,128,128]{2,1,0:T(8,128)S(1)} %copy-done.5, f32[128,128]{1,0:T(8,128)S(1)} %get-tuple-element.11, f32[128,128]{1,0:T(8,128)S(1)} %get-tuple-element.12, f32[128]{0:T(128)S(1)} %copy-done.9, f32[128,128]{1,0:T(8,128)S(1)} %add_rsqrt_fusion, ...), kind=kLoop, calls=%fused_computation.12 | loop fusion | flops 18874368 | bytes 17039872 | tf_op jit(solution)/shard_map/convert_element_type | solution.py:65
  (29 shorter events, 0.2 us)
Async XLA Ops:
  7.2 13.0 %copy-start = (bf16[4,128,64]{1,2,0:T(8,128)(2,1)S(1)}, bf16[4,128,64]{1,2,0:T(8,128)(2,1)}, u32[]{:S(2)}) copy-start(bf16[4,128,64]{1,2,0:T(8,128)(2,1)} %param.7) | copy-start | bytes 196612
  7.2 4.4 copy-start.10
  7.2 156.3 %all-gather.5.cloned.1.call-start = ((), (), s32[]{:S(2)}) async-start(), calls=%async_computation.2 | async-start | bytes 10485760 | tf_op jit(solution)/shard_map/all_gather | solution.py:32
  11.5 239.5 %all-gather.3.cloned.1.call-start = ((), (), s32[]{:S(2)}) async-start(), calls=%async_computation.1 | async-start | bytes 10485760 | tf_op jit(solution)/shard_map/all_gather | solution.py:37
  11.6 3.7 copy-start.2
  11.8 8.4 %copy-start.9 = (f32[128]{0:T(128)S(1)}, f32[128]{0:T(128)}, u32[]{:S(2)}) copy-start(f32[128]{0:T(128)} %param.6) | copy-start | bytes 1540
  24.9 5.9 copy-start.1
  33.4 439.6 %reduce-scatter.2.cloned.1.call-start = ((), (), s32[]{:S(2)}) async-start(), calls=%async_computation.3 | async-start | bytes 20971520 | tf_op jit(solution)/shard_map/reduce_scatter | solution.py:41
  319.2 272.9 %all-reduce.5.cloned.1.call-start = ((), (), s32[]{:S(2)}) async-start(), calls=%async_computation.5 | async-start | bytes 262144 | tf_op jit(solution)/shard_map/psum | solution.py:61
  473.1 8.0 %copy-start.3 = (bf16[128,128,128]{2,1,0:T(8,128)(2,1)S(1)}, bf16[128,128,128]{2,1,0:T(8,128)(2,1)}, u32[]{:S(2)}) copy-start(bf16[128,128,128]{2,1,0:T(8,128)(2,1)} %param.5) | copy-start | bytes 12582916
  473.1 8.0 %copy-start.6 = (bf16[1,128,64,128]{3,2,1,0:T(8,128)(2,1)S(1)}, bf16[1,128,64,128]{3,2,1,0:T(8,128)(2,1)}, u32[]{:S(2)}) copy-start(bf16[1,128,64,128]{3,2,1,0:T(8,128)(2,1)} %get-tuple-element.5) | copy-start | bytes 6291460
  479.1 1.3 copy-start.7
  479.1 2.0 copy-start.8
  486.6 144.6 %all-reduce.3.cloned.1.call-start = ((), (), s32[]{:S(2)}) async-start(), calls=%async_computation.4 | async-start | bytes 16777216 | tf_op jit(solution)/shard_map/psum | solution.py:54
  631.2 11.6 %copy-start.4 = (bf16[128,128,128]{2,1,0:T(8,128)(2,1)S(1)}, bf16[128,128,128]{2,1,0:T(8,128)(2,1)}, u32[]{:S(2)}) copy-start(bf16[128,128,128]{2,1,0:T(8,128)(2,1)} %param.5) | copy-start | bytes 12582916
  631.2 11.6 %copy-start.5 = (f32[128,128,128]{2,1,0:T(8,128)S(1)}, f32[128,128,128]{2,1,0:T(8,128)}, u32[]{:S(2)}) copy-start(f32[128,128,128]{2,1,0:T(8,128)} %all-reduce.3.cloned.1.call-done) | copy-start | bytes 25165828
Sparse Core Ops, SparseCore 0:
  11.6 151.8 all-gather.4
  165.4 85.6 all-gather.2
  319.3 153.7 reduce-scatter.1
  486.7 105.3 all-reduce.4
  594.4 36.6 all-reduce.2
where the time goes:
time: 668 us; the launch traced here: 660 us
  waiting for transfers between devices  502 us (75%)
  matrix products  55.9 us (8%)
  other arithmetic  49.3 us (7%)
  local copies, waits for them, and re-layouts  34.2 us (5%)
  between operations  14.9 us (2%)
    reduce_scatter x1, waiting for transfers between devices, on_device(): lax.psum_scatter(jnp.einsum('icj,ick->jck', panel_part, left_side, prefer...  154 us
    all_gather x1, waiting for transfers between devices, on_device(): row_panel = lax.all_gather(product_grad, 'ja', axis=2, tiled=True)  130 us
    psum x1, waiting for transfers between devices, on_device(): summed = lax.psum(grad_part, ('ia', 'ja'))  99 us
    all_gather x1, waiting for transfers between devices, on_device(): lax.all_gather(right_side, 'ia', axis=0, tiled=True)  87.5 us
    psum x1, waiting for transfers between devices, on_device(): normed_grad = lax.psum(input_part, 'col')  32.2 us
    dot_general x1, matrix products, on_device(): jnp.einsum('icj,jck->ick', panel_part, lax.all_gather(right_side, 'ia', a...  25.2 us
    dot_general x1, local copies, waits for them, and re-layouts, on_device(): jnp.einsum('icj,ick->jck', panel_part, left_side, preferred_element_type=...  16.6 us
    dot_general x1, matrix products, on_device(): jnp.einsum('icj,ick->jck', panel_part, left_side, preferred_element_type=...  14.1 us
  transfers between devices with their start and end apart: 5, of which 5 were waited for; matrix products, arithmetic and copies ran while one was open for 4% of the time, Pallas kernels for 0%

commit v1 on v0

--- a/solution.py
+++ b/solution.py
@@ -58,7 +58,7 @@
         - jnp.mean(scaled, axis=-1, keepdims=True)
         - unit_rows * jnp.mean(scaled * unit_rows, axis=-1, keepdims=True)
     )
-    summed = lax.psum(grad_part, ("ia", "ja"))
+    summed = lax.psum(lax.psum(grad_part, "ia"), "ja")
     squares = lax.psum(jnp.sum(summed * summed), "col")
     factor = jnp.minimum(1.0, CLIP_LIMIT * lax.rsqrt(squares + 1e-06))
     weight_grads = summed * factor

time: 668 us -> 642 us (0.961)
  waiting for transfers between devices: 502 us -> 476 us
    psum x1 -> x2, waiting for transfers between devices: 99 us -> 72.6 us  [on_device(): summed = lax.psum(lax.psum(grad_part, 'ia'), 'ja')]
  transfers between devices with their start and end apart: 5 -> 6, of which waited for: 5 -> 6; matrix products, arithmetic and copies ran while one was open for 4% -> 4% of each run, Pallas kernels for 0% -> 0%
where the time goes in v1:
time: 642 us; the launch traced here: 635 us
  waiting for transfers between devices  476 us (74%)
  matrix products  55.9 us (9%)
  other arithmetic  49.3 us (8%)
  local copies, waits for them, and re-layouts  34.2 us (5%)
  between operations  15.2 us (2%)
    reduce_scatter x1, waiting for transfers between devices, on_device(): lax.psum_scatter(jnp.einsum('icj,ick->jck', panel_part, left_side, prefer...  154 us
    all_gather x1, waiting for transfers between devices, on_device(): row_panel = lax.all_gather(product_grad, 'ja', axis=2, tiled=True)  130 us
    all_gather x1, waiting for transfers between devices, on_device(): lax.all_gather(right_side, 'ia', axis=0, tiled=True)  87.5 us
    psum x2, waiting for transfers between devices, on_device(): summed = lax.psum(lax.psum(grad_part, 'ia'), 'ja')  72.6 us
    psum x1, waiting for transfers between devices, on_device(): normed_grad = lax.psum(input_part, 'col')  32.8 us
    dot_general x1, matrix products, on_device(): jnp.einsum('icj,jck->ick', panel_part, lax.all_gather(right_side, 'ia', a...  25.2 us
    dot_general x1, local copies, waits for them, and re-layouts, on_device(): jnp.einsum('icj,ick->jck', panel_part, left_side, preferred_element_type=...  16.6 us
    dot_general x1, matrix products, on_device(): jnp.einsum('icj,ick->jck', panel_part, left_side, preferred_element_type=...  14.1 us
  transfers between devices with their start and end apart: 6, of which 6 were waited for; matrix products, arithmetic and copies ran while one was open for 4% of the time, Pallas kernels for 0%

profile of v1, /device:TPU:0, one launch (start us, length us, event | category | flops | bytes accessed | tf_op | source)
XLA Modules:
  0.0 634.9 jit_solution(7055038705030784188)
XLA Ops:
  7.2 4.3 copy.18
  11.5 0.0 all-gather.3.cloned.1.call-start
  11.6 0.1 fusion.41
  11.7 0.1 broadcast_multiply_fusion.1
  11.8 3.5 convert_reduce_fusion
  15.3 4.8 fusion.10
  20.2 4.7 convolution_bitcast_fusion
  24.9 5.9 copy-done.1
  30.8 2.6 multiply_convert_fusion.5
  33.4 0.5 reduce-scatter.2.cloned.1.call-start
  33.9 129.6 %all-gather.5.cloned.1.call-done = bf16[128,64,512]{2,0,1:T(8,128)(2,1)} async-done(((bf16[128,64,128]{2,0,1:T(8,128)(2,1)}), bf16[128,64,512]{2,0,1:T(8,128)(2,1)}) %all-gather.5.cloned.1.call-update) | async-done | bytes 8388624 | tf_op jit(solution)/shard_map/all_gather | solution.py:32
  163.5 87.5 %all-gather.3.cloned.1.call-done = bf16[512,64,128]{2,1,0:T(8,128)(2,1)} async-done(((bf16[128,64,128]{2,1,0:T(8,128)(2,1)}), bf16[512,64,128]{2,1,0:T(8,128)(2,1)}) %all-gather.3.cloned.1.call-update) | async-done | bytes 8388624 | tf_op jit(solution)/shard_map/all_gather | solution.py:37
  251.0 25.2 %fusion.11 = f32[64,128,128]{2,1,0:T(8,128)} fusion(bf16[128,64,512]{2,0,1:T(8,128)(2,1)} %all-gather.5.cloned.1.call-done, bf16[512,64,128]{2,1,0:T(8,128)(2,1)} %all-gather.3.cloned.1.call-done), kind=kOutput, calls=%fused_computation.15 | convolution fusion | flops 1073741824 | bytes 20971520 | tf_op jit(solution)/shard_map/icj,jck->ick/dot_general | solution.py:34
  276.2 5.4 copy.20
  281.6 6.8 %fusion.28 = (bf16[1,128,64,128]{3,2,1,0:T(8,128)(2,1)S(1)}, bf16[1,128,64,128]{3,2,1,0:T(8,128)(2,1)}, bf16[128,64,128]{2,1,0:T(8,128)(2,1)S(1)}) fusion(f32[64,128,128]{1,0,2:T(8,128)} %copy.20, f32[128,128]{1,0:T(8,128)S(1)} %broadcast_multiply_fusion.1, f32[4,128,64,128]{3,2,0,1:T(8,128)} %copy-done.1), kind=kLoop, calls=%fused_computation.43 | loop fusion | flops 14680064 | bytes 18939904 | tf_op jit(solution)/shard_map/stack | solution.py:49
  288.5 14.1 %fusion.32 = f32[64,128,512]{2,1,0:T(8,128)} fusion(bf16[128,64,512]{2,0,1:T(8,128)(2,1)} %all-gather.5.cloned.1.call-done, bf16[128,64,128]{2,1,0:T(8,128)(2,1)S(1)} %get-tuple-element.8), kind=kOutput, calls=%fused_computation.47 | convolution fusion | flops 1073741824 | bytes 27262976 | tf_op jit(solution)/shard_map/icj,ick->jck/dot_general | solution.py:42
  302.6 16.6 %copy.23 = f32[64,128,512]{1,0,2:T(8,128)} copy(f32[64,128,512]{2,1,0:T(8,128)} %fusion.32) | data formatting | bytes 33554432 | tf_op jit(solution)/shard_map/icj,ick->jck/dot_general | solution.py:42
  319.2 0.0 all-reduce.6.cloned.1.call-start
  319.2 153.8 %reduce-scatter.2.cloned.1.call-done = f32[128,64,128]{2,1,0:T(8,128)} async-done(((f32[512,64,128]{2,1,0:T(8,128)}), f32[128,64,128]{2,1,0:T(8,128)}) %reduce-scatter.2.cloned.1.call-update) | async-done | bytes 4194320 | tf_op jit(solution)/shard_map/reduce_scatter | solution.py:41
  473.1 6.0 fusion.30
  479.2 1.3 copy-done.7
  480.4 0.7 copy-done.8
  481.1 5.4 fusion.34
  486.6 42.3 %all-reduce.6.cloned.1.call-done = f32[4,128,64]{1,2,0:T(8,128)} async-done(((f32[4,128,64]{1,2,0:T(8,128)}), f32[4,128,64]{1,2,0:T(8,128)}) %all-reduce.6.cloned.1.call-update) | async-done | bytes 131088 | tf_op jit(solution)/shard_map/psum | solution.py:61
  529.0 6.5 %convolution_bitcast_fusion.1 = f32[128,128,128]{2,1,0:T(8,128)} fusion(bf16[1,128,64,128]{3,2,1,0:T(8,128)(2,1)} %copy-done.8, bf16[1,128,64,128]{3,2,1,0:T(8,128)(2,1)} %copy-done.7, bf16[1,128,64,128]{3,2,1,0:T(8,128)(2,1)} %get-tuple-element.5, bf16[1,128,64,128]{3,2,1,0:T(8,128)(2,1)S(1)} %get-tuple-element.4, bf16[4,128,64]{1,2,0:T(8,128)(2,1)S(1)} %copy-done), kind=kOutput, calls=%fused_computation.42 | convolution fusion | flops 1086324736 | bytes 16842752 | tf_op jit(solution)/shard_map/wick,wdc->ikd/dot_general | solution.py:51
  535.5 30.3 %all-reduce.8.cloned.1.call-done = f32[4,128,64]{1,2,0:T(8,128)} async-done(((f32[4,128,64]{1,2,0:T(8,128)}), f32[4,128,64]{1,2,0:T(8,128)}) %all-reduce.8.cloned.1.call-update) | async-done | bytes 131088 | tf_op jit(solution)/shard_map/psum | solution.py:61
  565.8 1.5 multiply_reduce_fusion.1
  567.3 3.1 psum.31
  571.1 1.6 broadcast_multiply_fusion
  572.7 32.8 %all-reduce.4.cloned.1.call-done = f32[128,128,128]{2,1,0:T(8,128)} async-done(((f32[128,128,128]{2,1,0:T(8,128)}), f32[128,128,128]{2,1,0:T(8,128)}) %all-reduce.4.cloned.1.call-update) | async-done | bytes 8388624 | tf_op jit(solution)/shard_map/psum | solution.py:54
  605.5 11.6 %multiply_reduce_fusion = (f32[128,128]{1,0:T(8,128)S(1)}, f32[128,128]{1,0:T(8,128)S(1)}) fusion(f32[128,128,128]{2,1,0:T(8,128)} %all-reduce.4.cloned.1.call-done, f32[128]{0:T(128)S(1)} %copy-done.9, f32[128,128]{1,0:T(8,128)S(1)} %add_rsqrt_fusion, f32[128,128]{1,0:T(8,128)S(1)} %broadcast_multiply_fusion.4, bf16[128,128,128]{2,1,0:T(8,128)(2,1)} %param.5), kind=kLoop, calls=%fused_computation.17 | loop fusion | flops 14647296 | bytes 12845568 | tf_op jit(solution)/shard_map/reduce_sum | solution.py:58
  617.1 10.7 %fusion.9 = bf16[128,128,128]{2,1,0:T(8,128)(2,1)} fusion(bf16[128,128,128]{2,1,0:T(8,128)(2,1)S(1)} %copy-done.4, f32[128,128,128]{2,1,0:T(8,128)S(1)} %copy-done.5, f32[128,128]{1,0:T(8,128)S(1)} %get-tuple-element.11, f32[128,128]{1,0:T(8,128)S(1)} %get-tuple-element.12, f32[128]{0:T(128)S(1)} %copy-done.9, f32[128,128]{1,0:T(8,128)S(1)} %add_rsqrt_fusion, ...), kind=kLoop, calls=%fused_computation.12 | loop fusion | flops 18874368 | bytes 17039872 | tf_op jit(solution)/shard_map/convert_element_type | solution.py:65
  (32 shorter events, 0.3 us)
Async XLA Ops:
  7.2 13.0 %copy-start = (bf16[4,128,64]{1,2,0:T(8,128)(2,1)S(1)}, bf16[4,128,64]{1,2,0:T(8,128)(2,1)}, u32[]{:S(2)}) copy-start(bf16[4,128,64]{1,2,0:T(8,128)(2,1)} %param.7) | copy-start | bytes 196612
  7.2 4.4 copy-start.10
  7.2 156.3 %all-gather.5.cloned.1.call-start = ((), (), s32[]{:S(2)}) async-start(), calls=%async_computation.2 | async-start | bytes 10485760 | tf_op jit(solution)/shard_map/all_gather | solution.py:32
  11.5 239.5 %all-gather.3.cloned.1.call-start = ((), (), s32[]{:S(2)}) async-start(), calls=%async_computation.1 | async-start | bytes 10485760 | tf_op jit(solution)/shard_map/all_gather | solution.py:37
  11.6 3.7 copy-start.2
  11.8 8.4 %copy-start.9 = (f32[128]{0:T(128)S(1)}, f32[128]{0:T(128)}, u32[]{:S(2)}) copy-start(f32[128]{0:T(128)} %param.6) | copy-start | bytes 1540
  24.9 5.9 copy-start.1
  33.4 439.6 %reduce-scatter.2.cloned.1.call-start = ((), (), s32[]{:S(2)}) async-start(), calls=%async_computation.3 | async-start | bytes 20971520 | tf_op jit(solution)/shard_map/reduce_scatter | solution.py:41
  319.2 209.7 %all-reduce.6.cloned.1.call-start = ((), (), s32[]{:S(2)}) async-start(), calls=%async_computation.5 | async-start | bytes 262144 | tf_op jit(solution)/shard_map/psum | solution.py:61
  473.1 8.0 %copy-start.3 = (bf16[128,128,128]{2,1,0:T(8,128)(2,1)S(1)}, bf16[128,128,128]{2,1,0:T(8,128)(2,1)}, u32[]{:S(2)}) copy-start(bf16[128,128,128]{2,1,0:T(8,128)(2,1)} %param.5) | copy-start | bytes 12582916
  473.1 8.0 %copy-start.6 = (bf16[1,128,64,128]{3,2,1,0:T(8,128)(2,1)S(1)}, bf16[1,128,64,128]{3,2,1,0:T(8,128)(2,1)}, u32[]{:S(2)}) copy-start(bf16[1,128,64,128]{3,2,1,0:T(8,128)(2,1)} %get-tuple-element.5) | copy-start | bytes 6291460
  479.1 1.3 copy-start.7
  479.1 2.0 copy-start.8
  486.6 79.2 %all-reduce.8.cloned.1.call-start = ((), (), s32[]{:S(2)}) async-start(), calls=%async_computation.6 | async-start | bytes 262144 | tf_op jit(solution)/shard_map/psum | solution.py:61
  529.0 76.5 %all-reduce.4.cloned.1.call-start = ((), (), s32[]{:S(2)}) async-start(), calls=%async_computation.4 | async-start | bytes 16777216 | tf_op jit(solution)/shard_map/psum | solution.py:54
  605.5 11.6 %copy-start.4 = (bf16[128,128,128]{2,1,0:T(8,128)(2,1)S(1)}, bf16[128,128,128]{2,1,0:T(8,128)(2,1)}, u32[]{:S(2)}) copy-start(bf16[128,128,128]{2,1,0:T(8,128)(2,1)} %param.5) | copy-start | bytes 12582916
  605.5 11.6 %copy-start.5 = (f32[128,128,128]{2,1,0:T(8,128)S(1)}, f32[128,128,128]{2,1,0:T(8,128)}, u32[]{:S(2)}) copy-start(f32[128,128,128]{2,1,0:T(8,128)} %all-reduce.4.cloned.1.call-done) | copy-start | bytes 25165828
Sparse Core Ops, SparseCore 0:
  11.6 151.8 all-gather.4
  165.4 85.6 all-gather.2
  319.3 153.7 reduce-scatter.1
  486.7 42.2 all-reduce.5
  531.1 34.6 all-reduce.7
  568.1 37.3 all-reduce.3
